TPU v7x, 32 devices: a whole 2x2x4 slice. The times are simulated.
32 devices in a mesh: comp: 2 (over core), blk: 16 (over z, y, x).
Axes of the slice: x: 2, y: 2, z: 4, core: 2. Of those that a mesh axis runs over, the one named last changes fastest.
Arguments:
- initial: float32 [2, 5, 128, 2048], P('comp', None, 'blk'), may hold values from -3 to 3
- ice_forcing: float32 [5, 128, 2048], P(None, 'blk'), may hold values from -2 to 4, as said below
- ocean_current: float32 [2, 128, 2048], P(None, 'blk'), may hold values from -1 to 1
- ice_cover: int32 [128, 2048], P('blk'), may hold values from 0 to 1, as said below
- targets: int32 [2, 128, 2048], P(None, 'blk'), may hold values from 0 to 32767, as said below
- weights: int32 [2, 128, 2048], P(None, 'blk'), may hold values from 1 to 4
Outputs:
- state_out: float32 [2, 5, 128, 2048], P('comp', None, 'blk')
- coupled: float32 [2, 3, 128, 2048], P('comp', None, 'blk')
Inputs may be any that keep to these rules, and one draw needn't show every extreme that they name: `ice_forcing`: channel 0 (mass) lies in 0.5 to 4, channel 1 (strength) and channel 4 (melt rate) in 0.2 to 2, channels 2 and 3 (wind stress) in -2 to 2. `ice_cover`: the share of ice-covered cells differs from strip to strip of 8 rows. `targets`: an entry of an ice cell at row r of its strip names an ocean row of the window no earlier than r.
All inputs are finite; a program needn't handle non-finite values.
Results may differ from a plain program's by a relative error of at most 0.0003.
Values sent between devices are 32-bit elements; how exact they have to be, the bound alone decides.
A program may use at most 128 MiB of HBM per device.

v0:
```python
import jax
import jax.numpy as jnp
from jax import lax
from jax.sharding import PartitionSpec as P

SUBCYCLES = 16


relax_rate = 0.5
ecc_sq = 4.0
delta_floor = 0.1
coriolis = 0.1
drag_coef = 1.0
inertia = 4.0
courant = 0.2
dilution = 0.5
weight_norm = 4.0
level_speed = (1.0, 0.8, 0.6, 0.45, 0.3)


def extended_2(block, sides, width):
    for axis, dim in sides:
        count = lax.axis_size(axis)
        forward = [(i, i + 1) for i in range(count - 1)]
        backward = [(target, source) for source, target in forward]
        low = lax.ppermute(
            lax.slice_in_dim(block, block.shape[dim] - width, None, axis=dim), axis, forward
        )
        high = lax.ppermute(lax.slice_in_dim(block, 0, width, axis=dim), axis, backward)
        block = jnp.concatenate([low, block, high], axis=dim)
    return block


def shifted(value, axis, steps):
    count = lax.axis_size(axis)
    first, last = (max(0, -steps), min(count, count - steps))
    return lax.ppermute(value, axis, [(source, source + steps) for source in range(first, last)])


def from_behind(value, axis, steps):
    count = lax.axis_size(axis)
    pairs = [(source, (source + steps) % count) for source in range(count)]
    return lax.ppermute(value, axis, pairs)


def along_rows(field):
    return 0.5 * (field[..., 2:, :] - field[..., :-2, :])


def across(field):
    padded = jnp.pad(field, [(0, 0)] * (field.ndim - 1) + [(1, 1)])
    return 0.5 * (padded[..., 2:] - padded[..., :-2])


def ice_step(fields, forcing, current, covered):
    vel_x = fields[0]
    vel_y = fields[1]
    strain_d = along_rows(vel_x) + across(vel_y[1:-1])
    strain_t = along_rows(vel_x) - across(vel_y[1:-1])
    strain_s = across(vel_x[1:-1]) + along_rows(vel_y)
    delta = jnp.sqrt(
        strain_d * strain_d
        + (strain_t * strain_t + strain_s * strain_s) / ecc_sq
        + delta_floor * delta_floor
    )
    press = forcing[1, 1:-1] * covered[1:-1]
    sig_one = (fields[2, 1:-1] + relax_rate * press * (strain_d / delta - 1.0)) / (1.0 + relax_rate)
    sig_two = (fields[3, 1:-1] + relax_rate * press * strain_t / (ecc_sq * delta)) / (
        1.0 + relax_rate
    )
    sig_shear = (fields[4, 1:-1] + relax_rate * press * strain_s / (2.0 * ecc_sq * delta)) / (
        1.0 + relax_rate
    )
    sig_xx = 0.5 * (sig_one + sig_two)
    sig_yy = 0.5 * (sig_one - sig_two)
    force_x = along_rows(sig_xx) + across(sig_shear[1:-1])
    force_y = along_rows(sig_shear) + across(sig_yy[1:-1])
    beta = inertia * forcing[0, 2:-2]
    old_x = vel_x[2:-2]
    old_y = vel_y[2:-2]
    denom = beta + drag_coef
    new_x = (
        covered[2:-2]
        * (
            beta * old_x
            + coriolis * beta * old_y
            + force_x
            + forcing[2, 2:-2]
            + drag_coef * current[0, 2:-2]
        )
        / denom
    )
    new_y = (
        covered[2:-2]
        * (
            beta * old_y
            - coriolis * beta * old_x
            + force_y
            + forcing[3, 2:-2]
            + drag_coef * current[1, 2:-2]
        )
        / denom
    )
    return jnp.stack([new_x, new_y, sig_one[1:-1], sig_two[1:-1], sig_shear[1:-1]])


def ocean_step(tracer, current):
    speed = jnp.asarray(level_speed, jnp.float32)[:, None, None]
    centre = tracer[:, 2:-2]
    below = centre - tracer[:, 1:-3]
    above = tracer[:, 3:-1] - centre
    padded = jnp.pad(centre, ((0, 0), (0, 0), (1, 1)))
    left_diff = centre - padded[:, :, :-2]
    right_diff = padded[:, :, 2:] - centre
    speed_x = speed * current[0, 2:-2][None]
    speed_y = speed * current[1, 2:-2][None]
    change = (
        jnp.maximum(speed_x, 0.0) * below
        + jnp.minimum(speed_x, 0.0) * above
        + jnp.maximum(speed_y, 0.0) * left_diff
        + jnp.minimum(speed_y, 0.0) * right_diff
    )
    return centre - courant * change


def coupling_terms(fields, forcing, current, covered):
    stress_x = covered * drag_coef * (fields[0] - current[0])
    stress_y = covered * drag_coef * (fields[1] - current[1])
    fresh = forcing[4] * covered * jnp.sqrt(1.0 + fields[0] * fields[0] + fields[1] * fields[1])
    return jnp.stack([stress_x, stress_y, fresh])


def remap_window(values, targets, weights):
    scaled = weights.astype(jnp.float32) / weight_norm
    window_size = 2 * values.shape[1] * values.shape[2]
    flat_targets = targets.reshape(-1)

    def spread(single):
        return jax.ops.segment_sum(
            (single[None] * scaled).reshape(-1), flat_targets, num_segments=window_size
        )

    return jax.vmap(spread)(values)


def body(initial, ice_forcing, ocean_current, ice_cover, targets, weights):
    depth = 2
    width = 2 * depth
    is_ice = lax.axis_index("comp") == 0
    row_count = initial.shape[2]
    col_count = initial.shape[3]
    covered = ice_cover.astype(jnp.float32)
    statics = jnp.concatenate([ice_forcing, ocean_current, covered[None]], axis=0)
    static_ext = extended_2(statics, (("blk", 1),), width)
    forcing_ext = static_ext[:5]
    current_ext = static_ext[5:7]
    cover_ext = static_ext[7]
    empty_total = jnp.zeros((3, row_count, col_count), jnp.float32)

    def ice_turns(extended):
        fields = extended
        total = empty_total
        for turn in range(depth):
            lower = 2 * turn
            upper = row_count + 2 * width - 2 * turn
            fields = ice_step(
                fields,
                forcing_ext[:, lower:upper],
                current_ext[:, lower:upper],
                cover_ext[lower:upper],
            )
            own_start = width - 2 * (turn + 1)
            own_fields = fields[:, own_start : own_start + row_count]
            total = total + coupling_terms(own_fields, ice_forcing, ocean_current, covered)
        return (fields, total)

    def ocean_turns(extended):
        fields = extended
        for turn in range(depth):
            lower = 2 * turn
            upper = row_count + 2 * width - 2 * turn
            fields = ocean_step(fields, current_ext[:, lower:upper])
        return (fields, empty_total)

    def advance(step_index, carry):
        fields, total = carry
        extended = extended_2(fields, (("blk", 1),), width)
        fields, extra = lax.cond(is_ice, ice_turns, ocean_turns, extended)
        return (fields, total + extra)

    fields, total = lax.fori_loop(0, SUBCYCLES // depth, advance, (initial[0], empty_total))
    average = total / SUBCYCLES
    empty_window = jnp.zeros((3, 2 * row_count * col_count), jnp.float32)

    def window_sums(values):
        return remap_window(values, targets, weights)

    def no_window(values):
        return empty_window

    partial_sums = lax.cond(is_ice, window_sums, no_window, average)
    window = shifted(partial_sums, "comp", 1)
    half_size = row_count * col_count
    from_before = from_behind(window[:, half_size:], "blk", 1)
    flux = (window[:, :half_size] + from_before).reshape(3, row_count, col_count)

    def ice_result(fields, flux):
        return (fields, average)

    def ocean_result(fields, flux):
        salinity = jnp.concatenate([fields[:1] - dilution * flux[2][None], fields[1:]], axis=0)
        return (salinity, flux)

    final_state, coupled = lax.cond(is_ice, ice_result, ocean_result, fields, flux)
    return (final_state[None], coupled[None])


def solution(mesh):
    placed = (
        P("comp", None, "blk", None),
        P(None, "blk", None),
        P(None, "blk", None),
        P("blk", None),
        P(None, "blk", None),
        P(None, "blk", None),
    )
    return jax.shard_map(
        body,
        mesh=mesh,
        in_specs=placed,
        out_specs=(P("comp", None, "blk", None), P("comp", None, "blk", None)),
        check_vma=False,
    )
```

profile of v0, /device:TPU:1, one launch (start us, length us, event | category | flops | bytes accessed | tf_op | source)
XLA Modules:
  0.0 408.0 jit_solution(8119902441815273502)
XLA Ops:
  0.6 1.7 copy.50
  4.4 3.9 collective-permute-start.2
  8.3 1.3 collective-permute-start.3
  9.7 3.6 collective-permute-done.2
  13.3 7.6 %collective-permute-done.3 = f32[8,4,2048]{2,1,0:T(4,128)S(1)} collective-permute-done((f32[8,4,2048]{2,1,0:T(4,128)S(1)}, f32[8,4,2048]{2,1,0:T(4,128)S(1)}, u32[]{:S(2)}, u32[]{:S(2)}) %collective-permute-start.3) | collective-permute-done | bytes 262176 | tf_op jit(solution)/shard_map/ppermute | solution.py:29
  23.0 124.8 %while.15 = (s32[]{:T(128)}, f32[5,8,2048]{2,1,0:T(8,128)}, f32[3,8,2048]{2,1,0:T(8,128)S(1)}, pred[]{:T(512)}, f32[2,16,2048]{2,1,0:T(8,128)S(1)}, /*index=5*/f...) while((s32[]{:T(128)}, f32[5,8,2048]{2,1,0:T(8,128)}, ...), condition=%wide.region_3.4_spmd.clone.clone.clone, body=%wide.region_0.3_spmd.sunk.clone.clone.clone.sunk | while | flops 4530180 | bytes 15696172 | solution.py:191
  23.0 1.2 fusion.106
  24.2 1.3 collective-permute-start
  25.5 4.0 collective-permute-start.1
  30.2 4.5 %collective-permute-done.1 = f32[5,4,2048]{2,1,0:T(4,128)S(1)} collective-permute-done((f32[5,4,2048]{2,1,0:T(4,128)S(1)}, f32[5,4,2048]{2,1,0:T(4,128)S(1)}, u32[]{:S(2)}, u32[]{:S(2)}) %collective-permute-start.1) | collective-permute-done | bytes 163872 | tf_op jit(solution)/shard_map/while/body/eval_jaxpr/ppermute | solution.py:26
  35.8 3.1 conditional.10
  35.9 1.2 fusion.74
  37.2 1.7 fusion.85
  40.2 1.3 collective-permute-start
  41.5 4.7 %collective-permute-start.1 = (f32[5,4,2048]{2,1,0:T(4,128)S(1)}, f32[5,4,2048]{2,1,0:T(4,128)S(1)}, u32[]{:S(2)}, u32[]{:S(2)}) collective-permute-start(f32[5,4,2048]{2,1,0:T(4,128)S(1)} %get-tuple-element.375), channel_id=1, source_target_pairs={{0,1},{1,2},{2,3},{3,4},{4,5},{5,6},{6,7},{7,8},{8,9},{9,10},{10,1... | collective-permute-start | bytes 491528 | tf_op jit(solution)/shard_map/while/body/eval_jaxpr/ppermute | solution.py:26
  47.0 1.5 collective-permute-done.1
  49.5 3.1 conditional.10
  49.7 1.2 fusion.74
  51.0 1.7 fusion.85
  53.9 1.3 collective-permute-start
  55.2 5.4 %collective-permute-start.1 = (f32[5,4,2048]{2,1,0:T(4,128)S(1)}, f32[5,4,2048]{2,1,0:T(4,128)S(1)}, u32[]{:S(2)}, u32[]{:S(2)}) collective-permute-start(f32[5,4,2048]{2,1,0:T(4,128)S(1)} %get-tuple-element.375), channel_id=1, source_target_pairs={{0,1},{1,2},{2,3},{3,4},{4,5},{5,6},{6,7},{7,8},{8,9},{9,10},{10,1... | collective-permute-start | bytes 491528 | tf_op jit(solution)/shard_map/while/body/eval_jaxpr/ppermute | solution.py:26
  61.3 2.2 collective-permute-done.1
  64.6 3.1 conditional.10
  64.7 1.2 fusion.74
  66.0 1.7 fusion.85
  69.0 1.3 collective-permute-start
  70.3 4.6 %collective-permute-start.1 = (f32[5,4,2048]{2,1,0:T(4,128)S(1)}, f32[5,4,2048]{2,1,0:T(4,128)S(1)}, u32[]{:S(2)}, u32[]{:S(2)}) collective-permute-start(f32[5,4,2048]{2,1,0:T(4,128)S(1)} %get-tuple-element.375), channel_id=1, source_target_pairs={{0,1},{1,2},{2,3},{3,4},{4,5},{5,6},{6,7},{7,8},{8,9},{9,10},{10,1... | collective-permute-start | bytes 491528 | tf_op jit(solution)/shard_map/while/body/eval_jaxpr/ppermute | solution.py:26
  75.7 4.3 %collective-permute-done.1 = f32[5,4,2048]{2,1,0:T(4,128)S(1)} collective-permute-done((f32[5,4,2048]{2,1,0:T(4,128)S(1)}, f32[5,4,2048]{2,1,0:T(4,128)S(1)}, u32[]{:S(2)}, u32[]{:S(2)}) %collective-permute-start.1) | collective-permute-done | bytes 163872 | tf_op jit(solution)/shard_map/while/body/eval_jaxpr/ppermute | solution.py:26
  81.1 3.1 conditional.10
  81.2 1.2 fusion.74
  82.5 1.7 fusion.85
  85.4 1.3 collective-permute-start
  86.7 4.4 %collective-permute-start.1 = (f32[5,4,2048]{2,1,0:T(4,128)S(1)}, f32[5,4,2048]{2,1,0:T(4,128)S(1)}, u32[]{:S(2)}, u32[]{:S(2)}) collective-permute-start(f32[5,4,2048]{2,1,0:T(4,128)S(1)} %get-tuple-element.375), channel_id=1, source_target_pairs={{0,1},{1,2},{2,3},{3,4},{4,5},{5,6},{6,7},{7,8},{8,9},{9,10},{10,1... | collective-permute-start | bytes 491528 | tf_op jit(solution)/shard_map/while/body/eval_jaxpr/ppermute | solution.py:26
  92.0 3.1 collective-permute-done.1
  96.1 3.1 conditional.10
  96.2 1.2 fusion.74
  97.5 1.7 fusion.85
  100.5 1.3 collective-permute-start
  101.8 6.7 %collective-permute-start.1 = (f32[5,4,2048]{2,1,0:T(4,128)S(1)}, f32[5,4,2048]{2,1,0:T(4,128)S(1)}, u32[]{:S(2)}, u32[]{:S(2)}) collective-permute-start(f32[5,4,2048]{2,1,0:T(4,128)S(1)} %get-tuple-element.375), channel_id=1, source_target_pairs={{0,1},{1,2},{2,3},{3,4},{4,5},{5,6},{6,7},{7,8},{8,9},{9,10},{10,1... | collective-permute-start | bytes 491528 | tf_op jit(solution)/shard_map/while/body/eval_jaxpr/ppermute | solution.py:26
  109.2 1.5 collective-permute-done.1
  111.8 3.1 conditional.10
  111.9 1.2 fusion.74
  113.2 1.7 fusion.85
  116.2 1.3 collective-permute-start
  117.5 4.9 %collective-permute-start.1 = (f32[5,4,2048]{2,1,0:T(4,128)S(1)}, f32[5,4,2048]{2,1,0:T(4,128)S(1)}, u32[]{:S(2)}, u32[]{:S(2)}) collective-permute-start(f32[5,4,2048]{2,1,0:T(4,128)S(1)} %get-tuple-element.375), channel_id=1, source_target_pairs={{0,1},{1,2},{2,3},{3,4},{4,5},{5,6},{6,7},{7,8},{8,9},{9,10},{10,1... | collective-permute-start | bytes 491528 | tf_op jit(solution)/shard_map/while/body/eval_jaxpr/ppermute | solution.py:26
  123.1 2.6 collective-permute-done.1
  126.9 3.1 conditional.10
  127.0 1.2 fusion.74
  128.3 1.7 fusion.85
  131.2 1.3 collective-permute-start
  132.5 4.4 %collective-permute-start.1 = (f32[5,4,2048]{2,1,0:T(4,128)S(1)}, f32[5,4,2048]{2,1,0:T(4,128)S(1)}, u32[]{:S(2)}, u32[]{:S(2)}) collective-permute-start(f32[5,4,2048]{2,1,0:T(4,128)S(1)} %get-tuple-element.375), channel_id=1, source_target_pairs={{0,1},{1,2},{2,3},{3,4},{4,5},{5,6},{6,7},{7,8},{8,9},{9,10},{10,1... | collective-permute-start | bytes 491528 | tf_op jit(solution)/shard_map/while/body/eval_jaxpr/ppermute | solution.py:26
  137.0 1.2 collective-permute-done
  138.2 5.3 %collective-permute-done.1 = f32[5,4,2048]{2,1,0:T(4,128)S(1)} collective-permute-done((f32[5,4,2048]{2,1,0:T(4,128)S(1)}, f32[5,4,2048]{2,1,0:T(4,128)S(1)}, u32[]{:S(2)}, u32[]{:S(2)}) %collective-permute-start.1) | collective-permute-done | bytes 163872 | tf_op jit(solution)/shard_map/while/body/eval_jaxpr/ppermute | solution.py:26
  144.5 3.1 conditional.10
  144.6 1.2 fusion.74
  145.9 1.7 fusion.85
  148.4 6.0 %conditional.3 = (f32[3,32768]{0,1:T(8,128)}) conditional(s32[]{:T(128)} %convert_element_type.31, () %tuple.38, (s32[2,8,2048]{2,1,0:T(8,128)S(1)}, f32[3,8,2048]{2,1,0:T(8,128)}, s32[2,8,2048]{2,1,0:T(8,128)S(1)}) %tuple.122), branch_computations={%region_4.5_spmd, %region_5.7_spmd} | conditional | flops 262144 | bytes 2686988 | solution.py:201
  148.4 6.0 %broadcast.141 = f32[3,32768]{0,1:T(8,128)} broadcast(f32[]{:T(128)} %constant.39.clone), dimensions={} | broadcast | bytes 393220 | tf_op jit(solution)/shard_map/broadcast.49
  154.4 9.5 %copy.17 = f32[3,32768]{1,0:T(4,128)S(1)} copy(f32[3,32768]{0,1:T(8,128)} %get-tuple-element.427) | data formatting | bytes 786432 | tf_op jit(solution)/shard_map/cond | solution.py:201
  163.9 1.3 collective-permute-start.4
  165.2 227.0 %collective-permute-done.4 = f32[3,32768]{1,0:T(4,128)S(1)} collective-permute-done((f32[3,32768]{1,0:T(4,128)S(1)}, f32[3,32768]{1,0:T(4,128)S(1)}, u32[]{:S(2)}, u32[]{:S(2)}) %collective-permute-start.4) | collective-permute-done | bytes 393248 | tf_op jit(solution)/shard_map/ppermute | solution.py:37
  392.3 2.3 collective-permute-start.5
  394.5 9.8 %collective-permute-done.5 = f32[3,16384]{1,0:T(4,128)S(1)} collective-permute-done((f32[3,16384]{1,0:T(4,128)S(1)}, f32[3,16384]{1,0:T(4,128)S(1)}, u32[]{:S(2)}, u32[]{:S(2)}) %collective-permute-start.5) | collective-permute-done | bytes 196640 | tf_op jit(solution)/shard_map/ppermute | solution.py:43
  404.3 3.7 conditional.4
  (90 shorter events, 32.2 us)
Async XLA Ops:
  4.4 8.9 %collective-permute-start.2 = (f32[8,4,2048]{2,1,0:T(4,128)S(1)}, f32[8,4,2048]{2,1,0:T(4,128)S(1)}, u32[]{:S(2)}, u32[]{:S(2)}) collective-permute-start(f32[8,4,2048]{2,1,0:T(4,128)S(1)} %get-tuple-element.305), channel_id=1, source_target_pairs={{0,1},{1,2},{2,3},{3,4},{4,5},{5,6},{6,7},{7,8},{8,9},{9,10},{10,1... | collective-permute-start | bytes 786440 | tf_op jit(solution)/shard_map/ppermute | solution.py:26
  8.3 12.5 %collective-permute-start.3 = (f32[8,4,2048]{2,1,0:T(4,128)S(1)}, f32[8,4,2048]{2,1,0:T(4,128)S(1)}, u32[]{:S(2)}, u32[]{:S(2)}) collective-permute-start(f32[8,4,2048]{2,1,0:T(4,128)S(1)} %get-tuple-element.306), channel_id=1, source_target_pairs={{1,0},{2,1},{3,2},{4,3},{5,4},{6,5},{7,6},{8,7},{9,8},{10,9},{11,1... | collective-permute-start | bytes 786440 | tf_op jit(solution)/shard_map/ppermute | solution.py:29
  23.0 125.5 %copy-start = (s32[2,8,2048]{2,1,0:T(8,128)S(1)}, s32[2,8,2048]{2,1,0:T(8,128)}, u32[]{:S(2)}) copy-start(s32[2,8,2048]{2,1,0:T(8,128)} %param.20) | copy-start | bytes 393220
  23.0 125.5 %copy-start.1 = (s32[2,8,2048]{2,1,0:T(8,128)S(1)}, s32[2,8,2048]{2,1,0:T(8,128)}, u32[]{:S(2)}) copy-start(s32[2,8,2048]{2,1,0:T(8,128)} %param.21) | copy-start | bytes 393220
  24.2 6.1 %collective-permute-start = (f32[5,4,2048]{2,1,0:T(4,128)S(1)}, f32[5,4,2048]{2,1,0:T(4,128)S(1)}, u32[]{:S(2)}, u32[]{:S(2)}) collective-permute-start(f32[5,4,2048]{2,1,0:T(4,128)S(1)} %get-tuple-element.374), channel_id=1, source_target_pairs={{1,0},{2,1},{3,2},{4,3},{5,4},{6,5},{7,6},{8,7},{9,8},{10,9},{11,1... | collective-permute-start | bytes 491528 | tf_op jit(solution)/shard_map/while/body/eval_jaxpr/ppermute | solution.py:29
  25.5 9.2 %collective-permute-start.1 = (f32[5,4,2048]{2,1,0:T(4,128)S(1)}, f32[5,4,2048]{2,1,0:T(4,128)S(1)}, u32[]{:S(2)}, u32[]{:S(2)}) collective-permute-start(f32[5,4,2048]{2,1,0:T(4,128)S(1)} %get-tuple-element.375), channel_id=1, source_target_pairs={{0,1},{1,2},{2,3},{3,4},{4,5},{5,6},{6,7},{7,8},{8,9},{9,10},{10,1... | collective-permute-start | bytes 491528 | tf_op jit(solution)/shard_map/while/body/eval_jaxpr/ppermute | solution.py:26
  40.2 6.8 %collective-permute-start = (f32[5,4,2048]{2,1,0:T(4,128)S(1)}, f32[5,4,2048]{2,1,0:T(4,128)S(1)}, u32[]{:S(2)}, u32[]{:S(2)}) collective-permute-start(f32[5,4,2048]{2,1,0:T(4,128)S(1)} %get-tuple-element.374), channel_id=1, source_target_pairs={{1,0},{2,1},{3,2},{4,3},{5,4},{6,5},{7,6},{8,7},{9,8},{10,9},{11,1... | collective-permute-start | bytes 491528 | tf_op jit(solution)/shard_map/while/body/eval_jaxpr/ppermute | solution.py:29
  41.5 7.0 %collective-permute-start.1 = (f32[5,4,2048]{2,1,0:T(4,128)S(1)}, f32[5,4,2048]{2,1,0:T(4,128)S(1)}, u32[]{:S(2)}, u32[]{:S(2)}) collective-permute-start(f32[5,4,2048]{2,1,0:T(4,128)S(1)} %get-tuple-element.375), channel_id=1, source_target_pairs={{0,1},{1,2},{2,3},{3,4},{4,5},{5,6},{6,7},{7,8},{8,9},{9,10},{10,1... | collective-permute-start | bytes 491528 | tf_op jit(solution)/shard_map/while/body/eval_jaxpr/ppermute | solution.py:26
  53.9 7.4 %collective-permute-start = (f32[5,4,2048]{2,1,0:T(4,128)S(1)}, f32[5,4,2048]{2,1,0:T(4,128)S(1)}, u32[]{:S(2)}, u32[]{:S(2)}) collective-permute-start(f32[5,4,2048]{2,1,0:T(4,128)S(1)} %get-tuple-element.374), channel_id=1, source_target_pairs={{1,0},{2,1},{3,2},{4,3},{5,4},{6,5},{7,6},{8,7},{9,8},{10,9},{11,1... | collective-permute-start | bytes 491528 | tf_op jit(solution)/shard_map/while/body/eval_jaxpr/ppermute | solution.py:29
  55.2 8.3 %collective-permute-start.1 = (f32[5,4,2048]{2,1,0:T(4,128)S(1)}, f32[5,4,2048]{2,1,0:T(4,128)S(1)}, u32[]{:S(2)}, u32[]{:S(2)}) collective-permute-start(f32[5,4,2048]{2,1,0:T(4,128)S(1)} %get-tuple-element.375), channel_id=1, source_target_pairs={{0,1},{1,2},{2,3},{3,4},{4,5},{5,6},{6,7},{7,8},{8,9},{9,10},{10,1... | collective-permute-start | bytes 491528 | tf_op jit(solution)/shard_map/while/body/eval_jaxpr/ppermute | solution.py:26
  69.0 6.7 %collective-permute-start = (f32[5,4,2048]{2,1,0:T(4,128)S(1)}, f32[5,4,2048]{2,1,0:T(4,128)S(1)}, u32[]{:S(2)}, u32[]{:S(2)}) collective-permute-start(f32[5,4,2048]{2,1,0:T(4,128)S(1)} %get-tuple-element.374), channel_id=1, source_target_pairs={{1,0},{2,1},{3,2},{4,3},{5,4},{6,5},{7,6},{8,7},{9,8},{10,9},{11,1... | collective-permute-start | bytes 491528 | tf_op jit(solution)/shard_map/while/body/eval_jaxpr/ppermute | solution.py:29
  70.3 9.7 %collective-permute-start.1 = (f32[5,4,2048]{2,1,0:T(4,128)S(1)}, f32[5,4,2048]{2,1,0:T(4,128)S(1)}, u32[]{:S(2)}, u32[]{:S(2)}) collective-permute-start(f32[5,4,2048]{2,1,0:T(4,128)S(1)} %get-tuple-element.375), channel_id=1, source_target_pairs={{0,1},{1,2},{2,3},{3,4},{4,5},{5,6},{6,7},{7,8},{8,9},{9,10},{10,1... | collective-permute-start | bytes 491528 | tf_op jit(solution)/shard_map/while/body/eval_jaxpr/ppermute | solution.py:26
  85.4 6.5 %collective-permute-start = (f32[5,4,2048]{2,1,0:T(4,128)S(1)}, f32[5,4,2048]{2,1,0:T(4,128)S(1)}, u32[]{:S(2)}, u32[]{:S(2)}) collective-permute-start(f32[5,4,2048]{2,1,0:T(4,128)S(1)} %get-tuple-element.374), channel_id=1, source_target_pairs={{1,0},{2,1},{3,2},{4,3},{5,4},{6,5},{7,6},{8,7},{9,8},{10,9},{11,1... | collective-permute-start | bytes 491528 | tf_op jit(solution)/shard_map/while/body/eval_jaxpr/ppermute | solution.py:29
  86.7 8.3 %collective-permute-start.1 = (f32[5,4,2048]{2,1,0:T(4,128)S(1)}, f32[5,4,2048]{2,1,0:T(4,128)S(1)}, u32[]{:S(2)}, u32[]{:S(2)}) collective-permute-start(f32[5,4,2048]{2,1,0:T(4,128)S(1)} %get-tuple-element.375), channel_id=1, source_target_pairs={{0,1},{1,2},{2,3},{3,4},{4,5},{5,6},{6,7},{7,8},{8,9},{9,10},{10,1... | collective-permute-start | bytes 491528 | tf_op jit(solution)/shard_map/while/body/eval_jaxpr/ppermute | solution.py:26
  100.5 8.7 %collective-permute-start = (f32[5,4,2048]{2,1,0:T(4,128)S(1)}, f32[5,4,2048]{2,1,0:T(4,128)S(1)}, u32[]{:S(2)}, u32[]{:S(2)}) collective-permute-start(f32[5,4,2048]{2,1,0:T(4,128)S(1)} %get-tuple-element.374), channel_id=1, source_target_pairs={{1,0},{2,1},{3,2},{4,3},{5,4},{6,5},{7,6},{8,7},{9,8},{10,9},{11,1... | collective-permute-start | bytes 491528 | tf_op jit(solution)/shard_map/while/body/eval_jaxpr/ppermute | solution.py:29
  101.8 8.9 %collective-permute-start.1 = (f32[5,4,2048]{2,1,0:T(4,128)S(1)}, f32[5,4,2048]{2,1,0:T(4,128)S(1)}, u32[]{:S(2)}, u32[]{:S(2)}) collective-permute-start(f32[5,4,2048]{2,1,0:T(4,128)S(1)} %get-tuple-element.375), channel_id=1, source_target_pairs={{0,1},{1,2},{2,3},{3,4},{4,5},{5,6},{6,7},{7,8},{8,9},{9,10},{10,1... | collective-permute-start | bytes 491528 | tf_op jit(solution)/shard_map/while/body/eval_jaxpr/ppermute | solution.py:26
  116.2 7.0 %collective-permute-start = (f32[5,4,2048]{2,1,0:T(4,128)S(1)}, f32[5,4,2048]{2,1,0:T(4,128)S(1)}, u32[]{:S(2)}, u32[]{:S(2)}) collective-permute-start(f32[5,4,2048]{2,1,0:T(4,128)S(1)} %get-tuple-element.374), channel_id=1, source_target_pairs={{1,0},{2,1},{3,2},{4,3},{5,4},{6,5},{7,6},{8,7},{9,8},{10,9},{11,1... | collective-permute-start | bytes 491528 | tf_op jit(solution)/shard_map/while/body/eval_jaxpr/ppermute | solution.py:29
  117.5 8.3 %collective-permute-start.1 = (f32[5,4,2048]{2,1,0:T(4,128)S(1)}, f32[5,4,2048]{2,1,0:T(4,128)S(1)}, u32[]{:S(2)}, u32[]{:S(2)}) collective-permute-start(f32[5,4,2048]{2,1,0:T(4,128)S(1)} %get-tuple-element.375), channel_id=1, source_target_pairs={{0,1},{1,2},{2,3},{3,4},{4,5},{5,6},{6,7},{7,8},{8,9},{9,10},{10,1... | collective-permute-start | bytes 491528 | tf_op jit(solution)/shard_map/while/body/eval_jaxpr/ppermute | solution.py:26
  131.2 6.9 %collective-permute-start = (f32[5,4,2048]{2,1,0:T(4,128)S(1)}, f32[5,4,2048]{2,1,0:T(4,128)S(1)}, u32[]{:S(2)}, u32[]{:S(2)}) collective-permute-start(f32[5,4,2048]{2,1,0:T(4,128)S(1)} %get-tuple-element.374), channel_id=1, source_target_pairs={{1,0},{2,1},{3,2},{4,3},{5,4},{6,5},{7,6},{8,7},{9,8},{10,9},{11,1... | collective-permute-start | bytes 491528 | tf_op jit(solution)/shard_map/while/body/eval_jaxpr/ppermute | solution.py:29
  132.5 10.9 %collective-permute-start.1 = (f32[5,4,2048]{2,1,0:T(4,128)S(1)}, f32[5,4,2048]{2,1,0:T(4,128)S(1)}, u32[]{:S(2)}, u32[]{:S(2)}) collective-permute-start(f32[5,4,2048]{2,1,0:T(4,128)S(1)} %get-tuple-element.375), channel_id=1, source_target_pairs={{0,1},{1,2},{2,3},{3,4},{4,5},{5,6},{6,7},{7,8},{8,9},{9,10},{10,1... | collective-permute-start | bytes 491528 | tf_op jit(solution)/shard_map/while/body/eval_jaxpr/ppermute | solution.py:26
  163.9 228.3 %collective-permute-start.4 = (f32[3,32768]{1,0:T(4,128)S(1)}, f32[3,32768]{1,0:T(4,128)S(1)}, u32[]{:S(2)}, u32[]{:S(2)}) collective-permute-start(f32[3,32768]{1,0:T(4,128)S(1)} %copy.17), channel_id=1, source_target_pairs={{0,16},{1,17},{2,18},{3,19},{4,20},{5,21},{6,22},{7,23},{8,24},{9,... | collective-permute-start | bytes 1179656 | tf_op jit(solution)/shard_map/ppermute | solution.py:37
  392.3 12.1 %collective-permute-start.5 = (f32[3,16384]{1,0:T(4,128)S(1)}, f32[3,16384]{1,0:T(4,128)S(1)}, u32[]{:S(2)}, u32[]{:S(2)}) collective-permute-start(f32[3,16384]{1,0:T(4,128)S(1)} %slice.432), channel_id=1, source_target_pairs={{0,1},{1,2},{2,3},{3,4},{4,5},{5,6},{6,7},{7,8},{8,9},{9,10},{10,1... | collective-permute-start | bytes 589832 | tf_op jit(solution)/shard_map/ppermute | solution.py:43
where the time goes:
time: 412 us; the launch traced here: 408 us
  waiting for transfers between devices  279 us (68%)
  starting transfers between devices  58.3 us (14%)
  other arithmetic  39.1 us (9%)
  local copies, waits for them, and re-layouts  29.5 us (7%)
    ppermute x1, waiting for transfers between devices, shifted(): lax.ppermute(value, axis, [(source, source + steps) for source in range(f...  227 us
    ppermute x9, starting transfers between devices, extended_2(): lax.ppermute(lax.slice_in_dim(block, block.shape[dim] - width, None, axis...  43.1 us
    ppermute x9, waiting for transfers between devices, extended_2(): lax.ppermute(lax.slice_in_dim(block, block.shape[dim] - width, None, axis...  28.5 us
    sub x16, other arithmetic, ocean_step(): return centre - courant * change  23.4 us
    ppermute x9, waiting for transfers between devices, extended_2(): lax.ppermute(lax.slice_in_dim(block, 0, width, axis=dim), axis, backward)  14.1 us
    ppermute x9, starting transfers between devices, extended_2(): lax.ppermute(lax.slice_in_dim(block, 0, width, axis=dim), axis, backward)  11.6 us
    ppermute x1, waiting for transfers between devices, from_behind(): return lax.ppermute(value, axis, pairs)  9.83 us
    concatenate x9, other arithmetic, extended_2(): block = jnp.concatenate([low, block, high], axis=dim)  9.76 us
  transfers between devices with their start and end apart: 20, of which 20 were waited for; matrix products, arithmetic and copies ran while one was open for 0% of the time, Pallas kernels for 0%

commit v1 on v0

v1 whole, which is shorter than its diff:
```python
import functools

import jax
import jax.numpy as jnp
from jax import lax
from jax.experimental import pallas as pl
from jax.experimental.pallas import tpu as pltpu
from jax.sharding import PartitionSpec as P

SUBCYCLES = 16
MESH = pl.DeviceIdType.MESH
PAD = 128

coriolis = 0.1
inertia = 4.0
courant = 0.2
dilution = 0.5
weight_norm = 4.0
level_speed = (1.0, 0.8, 0.6, 0.45, 0.3)


def rolled(value, steps, axis):
    return pltpu.roll(value, steps % value.shape[axis], axis)


def rows_diff(value):
    return rolled(value, -1, 0) - rolled(value, 1, 0)


def chunk_width(cols):
    return 256 if cols % 256 == 0 else 128


def stress_stage(work, stat, start, width):
    wide = pl.ds(start, width + 2 * PAD)
    mid = pl.ds(start + PAD, width)
    inner = slice(PAD, PAD + width)
    vel_x, vel_y = work[0, :, wide], work[1, :, wide]
    cx = (rolled(vel_x, -1, 1) - rolled(vel_x, 1, 1))[:, inner]
    cy = (rolled(vel_y, -1, 1) - rolled(vel_y, 1, 1))[:, inner]
    rx = rows_diff(vel_x[:, inner])
    ry = rows_diff(vel_y[:, inner])
    e_d = rx + cy
    e_t = rx - cy
    e_s = cx + ry
    inv = lax.rsqrt(0.25 * (e_d * e_d) + 0.0625 * (e_t * e_t + e_s * e_s) + 0.01)
    third = stat[0, :, pl.ds(start, width)]
    scaled = third * inv
    work[2, :, mid] = work[2, :, mid] * (2.0 / 3.0) + (0.5 * scaled * e_d - third)
    work[3, :, mid] = work[3, :, mid] * (2.0 / 3.0) + 0.125 * scaled * e_t
    work[4, :, mid] = work[4, :, mid] * (2.0 / 3.0) + 0.0625 * scaled * e_s


def velocity_stage(work, stat, total, start, width, rows):
    wide = pl.ds(start, width + 2 * PAD)
    mid = pl.ds(start + PAD, width)
    here = pl.ds(start, width)
    inner = slice(PAD, PAD + width)
    shear = work[4, :, wide]
    one, two = work[2, :, wide], work[3, :, wide]
    across_shear = (rolled(shear, -1, 1) - rolled(shear, 1, 1))[:, inner]
    lower = one - two
    across_yy = (rolled(lower, -1, 1) - rolled(lower, 1, 1))[:, inner]
    force_x = rows_diff((one + two)[:, inner]) + 2.0 * across_shear
    force_y = 2.0 * rows_diff(shear[:, inner]) + across_yy
    old_x, old_y = work[0, :, mid], work[1, :, mid]
    keep, push = stat[1, :, here], stat[2, :, here]
    new_x = keep * (old_x + coriolis * old_y) + push * force_x + stat[3, :, here]
    new_y = keep * (old_y - coriolis * old_x) + push * force_y + stat[4, :, here]
    work[0, :, mid] = new_x
    work[1, :, mid] = new_y
    own_x, own_y = new_x[rows : 2 * rows], new_y[rows : 2 * rows]
    total[0, :, here] += own_x
    total[1, :, here] += own_y
    total[2, :, here] += jnp.sqrt(1.0 + own_x * own_x + own_y * own_y)


def ocean_stage(source, target, coef, start, width):
    wide = pl.ds(start, width + 2 * PAD)
    mid = pl.ds(start + PAD, width)
    here = pl.ds(start, width)
    inner = slice(PAD, PAD + width)
    up, down, east, west = (coef[i, :, here] for i in range(4))
    for level, speed in enumerate(level_speed):
        tracer = source[level, :, wide]
        centre = tracer[:, inner]
        right = rolled(tracer, -1, 1)[:, inner] - centre
        left = centre - rolled(tracer, 1, 1)[:, inner]
        above = rolled(centre, -1, 0) - centre
        below = centre - rolled(centre, 1, 0)
        change = up * below + down * above + east * left + west * right
        target[level, :, mid] = centre - speed * change


def turns_kernel(
    initial, forcing, current, cover, state, average,
    own, own_stat, halo, halo_stat, work, spare, stat, total, mean,
    send, recv, stat_send, stat_recv, mean_send, mean_recv,
):
    me = lax.axis_index("blk")
    comp = lax.axis_index("comp")
    count = lax.axis_size("blk")
    fields, rows, cols = initial.shape
    width = chunk_width(cols)
    chunks = cols // width
    right, left = lax.rem(me + 1, count), lax.rem(me + count - 1, count)
    has_left, has_right = me > 0, me < count - 1

    barrier = pltpu.get_barrier_semaphore()
    pl.semaphore_signal(barrier, inc=1, device_id={"blk": right}, device_id_type=MESH)
    pl.semaphore_signal(barrier, inc=1, device_id={"blk": left}, device_id_type=MESH)
    pl.semaphore_signal(barrier, inc=1, device_id={"comp": 1 - comp}, device_id_type=MESH)

    work[...] = jnp.zeros_like(work)
    spare[...] = jnp.zeros_like(spare)
    total[...] = jnp.zeros_like(total)
    covered = cover[...].astype(jnp.float32)

    def copies(source, target, out_sem, in_sem):
        up = pltpu.make_async_remote_copy(
            source, target.at[0], out_sem.at[0], in_sem.at[0],
            device_id={"blk": right}, device_id_type=MESH,
        )
        down = pltpu.make_async_remote_copy(
            source, target.at[1], out_sem.at[1], in_sem.at[1],
            device_id={"blk": left}, device_id_type=MESH,
        )
        return up, down

    def start(pair):
        pl.when(has_right)(pair[0].start)
        pl.when(has_left)(pair[1].start)

    def arrive(pair):
        pl.when(has_left)(pair[0].wait_recv)
        pl.when(has_right)(pair[1].wait_recv)

    def sent(pair):
        pl.when(has_right)(pair[0].wait_send)
        pl.when(has_left)(pair[1].wait_send)

    def clear_edges(turns):
        @pl.when(jnp.logical_not(has_left))
        def _():
            halo_stat[0] = jnp.zeros_like(halo_stat[0])
            for turn in range(turns):
                halo[turn, 0] = jnp.zeros_like(halo[turn, 0])

        @pl.when(jnp.logical_not(has_right))
        def _():
            halo_stat[1] = jnp.zeros_like(halo_stat[1])
            for turn in range(turns):
                halo[turn, 1] = jnp.zeros_like(halo[turn, 1])

    inside = slice(PAD, PAD + cols)

    def fill(turn, source):
        for field in range(fields):
            work[field, 0:rows, inside] = halo[turn, 0, field]
            work[field, rows : 2 * rows, inside] = source[field]
            work[field, 2 * rows : 3 * rows, inside] = halo[turn, 1, field]

    mean_copy = pltpu.make_async_remote_copy(
        mean, average, mean_send, mean_recv,
        device_id={"comp": 1 - comp}, device_id_type=MESH,
    )

    @pl.when(comp == 0)
    def _():
        depth = rows // 2
        turns = SUBCYCLES // depth
        clear_edges(turns)
        push = covered / (inertia * forcing[0] + 1.0)
        own_stat[0] = forcing[1] * covered * (1.0 / 3.0)
        own_stat[1] = push
        own_stat[2] = push * (forcing[2] + current[0])
        own_stat[3] = push * (forcing[3] + current[1])
        pl.semaphore_wait(barrier, 3)
        stat_pair = copies(own_stat, halo_stat, stat_send, stat_recv)
        start(stat_pair)
        pairs = []
        for turn in range(turns):
            source = initial if turn == 0 else own.at[turn - 1]
            pair = copies(source, halo.at[turn], send.at[turn], recv.at[turn])
            pairs.append(pair)
            start(pair)
            if turn == 0:
                arrive(stat_pair)
                for place, block in enumerate((halo_stat.at[0], own_stat, halo_stat.at[1])):
                    span = slice(place * rows, (place + 1) * rows)
                    push = block[1]
                    stat[0, span] = block[0]
                    stat[1, span] = jnp.where(push > 0.0, 1.0 - push, 0.0)
                    stat[2, span] = 0.25 * push
                    stat[3, span] = block[2]
                    stat[4, span] = block[3]
            arrive(pair)
            fill(turn, source)

            def subcycle(step, carry):
                for chunk in range(chunks):
                    stress_stage(work, stat, chunk * width, width)
                for chunk in range(chunks):
                    velocity_stage(work, stat, total, chunk * width, width, rows)
                return carry

            lax.fori_loop(0, depth, subcycle, 0)
            final = state if turn == turns - 1 else own.at[turn]
            for field in range(fields):
                final[field] = work[field, rows : 2 * rows, inside]
        share = 1.0 / SUBCYCLES
        mean[0] = total[0] * share - covered * current[0]
        mean[1] = total[1] * share - covered * current[1]
        mean[2] = forcing[4] * covered * (total[2] * share)
        mean_copy.start()
        average[...] = mean[...]
        sent(stat_pair)
        for pair in pairs:
            sent(pair)
        mean_copy.wait_send()

    @pl.when(comp == 1)
    def _():
        depth = rows
        turns = SUBCYCLES // depth
        clear_edges(turns)
        pl.semaphore_wait(barrier, 3)
        stat_pair = copies(current, halo_stat.at[:, pl.ds(0, 2)], stat_send, stat_recv)
        start(stat_pair)
        pairs = []
        for turn in range(turns):
            source = initial if turn == 0 else own.at[turn - 1]
            pair = copies(source, halo.at[turn], send.at[turn], recv.at[turn])
            pairs.append(pair)
            start(pair)
            if turn == 0:
                arrive(stat_pair)
                for place in range(3):
                    span = slice(place * rows, (place + 1) * rows)
                    for axis in range(2):
                        if place == 1:
                            speed = current[axis]
                        else:
                            speed = halo_stat[place // 2, axis]
                        stat[2 * axis, span] = courant * jnp.maximum(speed, 0.0)
                        stat[2 * axis + 1, span] = courant * jnp.minimum(speed, 0.0)
            arrive(pair)
            fill(turn, source)

            def substeps(step, carry):
                for chunk in range(chunks):
                    ocean_stage(work, spare, stat, chunk * width, width)
                for chunk in range(chunks):
                    ocean_stage(spare, work, stat, chunk * width, width)
                return carry

            lax.fori_loop(0, depth // 2, substeps, 0)
            final = state if turn == turns - 1 else own.at[turn]
            for field in range(fields):
                final[field] = work[field, rows : 2 * rows, inside]
        sent(stat_pair)
        for pair in pairs:
            sent(pair)
        mean_copy.wait_recv()


def run_turns(initial, forcing, current, cover):
    fields, rows, cols = initial.shape
    most = SUBCYCLES // (rows // 2)
    f32 = jnp.float32
    vmem = pl.BlockSpec(memory_space=pltpu.VMEM)
    dma = pltpu.SemaphoreType.DMA
    return pl.pallas_call(
        turns_kernel,
        out_shape=(
            jax.ShapeDtypeStruct((fields, rows, cols), f32),
            jax.ShapeDtypeStruct((3, rows, cols), f32),
        ),
        in_specs=[vmem] * 4,
        out_specs=(vmem, vmem),
        scratch_shapes=[
            pltpu.VMEM((most, fields, rows, cols), f32),
            pltpu.VMEM((4, rows, cols), f32),
            pltpu.VMEM((most, 2, fields, rows, cols), f32),
            pltpu.VMEM((2, 4, rows, cols), f32),
            pltpu.VMEM((fields, 3 * rows, cols + 2 * PAD), f32),
            pltpu.VMEM((fields, 3 * rows, cols + 2 * PAD), f32),
            pltpu.VMEM((5, 3 * rows, cols), f32),
            pltpu.VMEM((3, rows, cols), f32),
            pltpu.VMEM((3, rows, cols), f32),
            dma((most, 2)), dma((most, 2)), dma((2,)), dma((2,)), dma, dma,
        ],
        compiler_params=pltpu.CompilerParams(
            collective_id=0, has_side_effects=True, vmem_limit_bytes=40 * 1024 * 1024
        ),
        name="turns",
    )(initial, forcing, current, cover)


def remap_kernel(average, targets, weights, window, acc, low_index, high_index):
    comp = lax.axis_index("comp")
    channels, rows, cols = average.shape
    span = low_index.shape[1]
    low_count, high_count = low_index.shape[0], high_index.shape[0]
    bf16 = jnp.bfloat16
    blocks = cols // low_count
    low_index[...] = lax.broadcasted_iota(jnp.int32, low_index.shape, 0).astype(bf16)
    high_index[...] = lax.broadcasted_iota(jnp.int32, high_index.shape, 0).astype(bf16)
    acc[...] = jnp.zeros_like(acc)

    def one_row(row, carry):
        for piece in range(cols // span):
            place = pl.ds(piece * span, span)
            target = targets[comp, pl.ds(row, 1), place]
            scale = weights[comp, pl.ds(row, 1), place].astype(jnp.float32) * (1.0 / weight_norm)
            low = lax.rem(target, low_count)
            block = lax.rem(lax.div(target, low_count), blocks)
            line = lax.div(target, cols)
            high = (lax.div(line, rows) * blocks + block) * rows + lax.rem(line, rows)
            low_hot = jnp.where(low_index[...] == low.astype(bf16), bf16(1), bf16(0))
            match = high_index[...] == high.astype(bf16)
            parts = []
            for channel in range(channels):
                value = average[channel, pl.ds(row, 1), place] * scale
                coarse = value.astype(bf16)
                fine = (value - coarse.astype(jnp.float32)).astype(bf16)
                parts.append(jnp.where(match, coarse, bf16(0)))
                parts.append(jnp.where(match, fine, bf16(0)))
            spread = jnp.concatenate(parts, axis=0)
            acc[...] += lax.dot_general(
                spread, low_hot, (((1,), (1,)), ((), ())), preferred_element_type=jnp.float32
            )
        return carry

    lax.fori_loop(0, rows, one_row, 0)
    for channel in range(channels):
        for half in range(2):
            for block in range(blocks):
                base = 2 * channel * high_count + (half * blocks + block) * rows
                window[channel, half, :, block * low_count : (block + 1) * low_count] = (
                    acc[base : base + rows] + acc[base + high_count : base + high_count + rows]
                )


def run_remap(average, targets, weights):
    channels, rows, cols = average.shape
    low_count = 256 if cols % 256 == 0 else 128
    high_count = 2 * rows * cols // low_count
    span = min(1024, cols)
    vmem = pl.BlockSpec(memory_space=pltpu.VMEM)
    return pl.pallas_call(
        remap_kernel,
        out_shape=jax.ShapeDtypeStruct((channels, 2, rows, cols), jnp.float32),
        in_specs=[vmem] * 3,
        out_specs=vmem,
        scratch_shapes=[
            pltpu.VMEM((2 * channels * high_count, low_count), jnp.float32),
            pltpu.VMEM((low_count, span), jnp.bfloat16),
            pltpu.VMEM((high_count, span), jnp.bfloat16),
        ],
        compiler_params=pltpu.CompilerParams(vmem_limit_bytes=40 * 1024 * 1024),
        name="remap",
    )(average, targets, weights)


def join_kernel(
    window, state, average, out_state, out_pair, beside, carry, before,
    side_send, side_recv, next_send, next_recv,
):
    me = lax.axis_index("blk")
    comp = lax.axis_index("comp")
    count = lax.axis_size("blk")
    right, left = lax.rem(me + 1, count), lax.rem(me + count - 1, count)
    barrier = pltpu.get_barrier_semaphore()
    pl.semaphore_signal(barrier, inc=1, device_id={"blk": right}, device_id_type=MESH)
    pl.semaphore_signal(barrier, inc=1, device_id={"blk": left}, device_id_type=MESH)
    pl.semaphore_signal(barrier, inc=1, device_id={"comp": 1 - comp}, device_id_type=MESH)
    pl.semaphore_wait(barrier, 3)
    side = pltpu.make_async_remote_copy(
        window, beside, side_send, side_recv,
        device_id={"comp": 1 - comp}, device_id_type=MESH,
    )
    onward = pltpu.make_async_remote_copy(
        carry, before, next_send, next_recv, device_id={"blk": right}, device_id_type=MESH
    )

    @pl.when(comp == 0)
    def _():
        side.start()
        out_state[...] = state[...]
        out_pair[...] = average[...]
        side.wait_send()

    @pl.when(comp == 1)
    def _():
        side.wait_recv()
        carry[...] = window[:, 1] + beside[:, 1]
        onward.start()
        out_pair[...] = window[:, 0] + beside[:, 0]
        out_state[...] = state[...]
        onward.wait_recv()
        out_pair[...] += before[...]
        out_state[0] -= dilution * out_pair[2]
        onward.wait_send()


def run_join(window, state, average):
    channels, rows, cols = average.shape
    vmem = pl.BlockSpec(memory_space=pltpu.VMEM)
    dma = pltpu.SemaphoreType.DMA
    return pl.pallas_call(
        join_kernel,
        out_shape=(
            jax.ShapeDtypeStruct(state.shape, jnp.float32),
            jax.ShapeDtypeStruct(average.shape, jnp.float32),
        ),
        in_specs=[vmem] * 3,
        out_specs=(vmem, vmem),
        scratch_shapes=[
            pltpu.VMEM(window.shape, jnp.float32),
            pltpu.VMEM(average.shape, jnp.float32),
            pltpu.VMEM(average.shape, jnp.float32),
            dma, dma, dma, dma,
        ],
        compiler_params=pltpu.CompilerParams(
            collective_id=1, has_side_effects=True, vmem_limit_bytes=40 * 1024 * 1024
        ),
        name="join",
    )(window, state, average)


def body(initial, ice_forcing, ocean_current, ice_cover, targets, weights):
    state, average = run_turns(initial[0], ice_forcing, ocean_current, ice_cover)
    window = run_remap(average, targets, weights)
    state, coupled = run_join(window, state, average)
    return (state[None], coupled[None])


def solution(mesh):
    placed = (
        P("comp", None, "blk", None),
        P(None, "blk", None),
        P(None, "blk", None),
        P("blk", None),
        P(None, "blk", None),
        P(None, "blk", None),
    )
    return jax.shard_map(
        body,
        mesh=mesh,
        in_specs=placed,
        out_specs=(P("comp", None, "blk", None), P("comp", None, "blk", None)),
        check_vma=False,
    )
```

time: 412 us -> 104 us (0.25)
  the two profiles are of different devices: /device:TPU:1 before, /device:TPU:11 now
where the time goes in v1:
time: 104 us
  Pallas kernels  98.4 us (95%)
  local copies, waits for them, and re-layouts  5.09 us (5%)
    pallas_call x1, Pallas kernels, run_turns(): pl.pallas_call(turns_kernel, out_shape=(jax.ShapeDtypeStruct((fields, row...  83.7 us
    pallas_call x1, Pallas kernels, run_remap(): pl.pallas_call(remap_kernel, out_shape=jax.ShapeDtypeStruct((channels, 2,...  8.42 us
    pallas_call x1, Pallas kernels, run_join(): pl.pallas_call(join_kernel, out_shape=(jax.ShapeDtypeStruct(state.shape,...  6.27 us
    unnamed x14, local copies, waits for them, and re-layouts  5.09 us

profile of v1, /device:TPU:11, one launch (start us, length us, event | category | flops | bytes accessed | tf_op | source)
XLA Modules:
  0.0 104.2 jit_solution(10889906028535468120)
XLA Ops:
  0.6 0.0 copy-start
  0.6 1.0 copy-done
  1.6 0.0 copy-start.1
  1.6 1.0 copy-done.1
  2.6 0.0 copy-start.2
  2.6 0.9 copy-done.2
  3.5 0.0 copy-start.5
  3.5 0.8 copy-done.5
  4.3 0.0 copy-start.3
  4.3 0.0 copy-start.4
  4.3 83.7 %turns.1 = (f32[5,8,2048]{2,1,0:T(8,128)S(1)}, f32[3,8,2048]{2,1,0:T(8,128)S(1)}) custom-call(f32[5,8,2048]{2,1,0:T(8,128)S(1)} %bitcast.3, f32[5,8,2048]{2,1,0:T(8,128)S(1)} %copy-done.1, f32[2,8,2048]{2,1,0:T(8,128)S(1)} %copy-done.2, s32[8,2048]{1,0:T(8,128)S(1)} %copy-done.5), custom_call_target="tpu_custom_call" | custom-call | tf_op jit(solution)/shard_map/turns/pallas_call | solution.py:273
  88.0 0.0 copy-done.3
  88.0 0.0 copy-done.4
  88.1 8.4 %remap.1.window = f32[3,2,8,2048]{3,2,1,0:T(8,128)S(1)} custom-call(f32[3,8,2048]{2,1,0:T(8,128)S(1)} %get-tuple-element.6.average, s32[2,8,2048]{2,1,0:T(8,128)S(1)} %copy-done.3, s32[2,8,2048]{2,1,0:T(8,128)S(1)} %copy-done.4), custom_call_target="tpu_custom_call" | custom-call | tf_op jit(solution)/shard_map/remap/pallas_call | solution.py:351
  96.5 6.3 %join.1 = (f32[5,8,2048]{2,1,0:T(8,128)S(1)}, f32[3,8,2048]{2,1,0:T(8,128)S(1)}) custom-call(f32[3,2,8,2048]{3,2,1,0:T(8,128)S(1)} %remap.1.window, f32[5,8,2048]{2,1,0:T(8,128)S(1)} %get-tuple-element.7.state, f32[3,8,2048]{2,1,0:T(8,128)S(1)} %get-tuple-element.6.average), custom_call_target="tpu_custom_call" | custom-call | tf_op jit(solution)/shard_map/join/pallas_call | solution.py:411
  102.8 0.7 copy.10
  103.5 0.7 copy.11
Async XLA Ops:
  0.6 1.0 copy-start
  1.6 1.0 copy-start.1
  2.6 0.9 copy-start.2
  3.5 0.8 copy-start.5
  4.3 83.7 %copy-start.3 = (s32[2,8,2048]{2,1,0:T(8,128)S(1)}, s32[2,8,2048]{2,1,0:T(8,128)}, u32[]{:S(2)}) copy-start(s32[2,8,2048]{2,1,0:T(8,128)} %targets.1) | copy-start | bytes 393220
  4.3 83.7 %copy-start.4 = (s32[2,8,2048]{2,1,0:T(8,128)S(1)}, s32[2,8,2048]{2,1,0:T(8,128)}, u32[]{:S(2)}) copy-start(s32[2,8,2048]{2,1,0:T(8,128)} %weights.1) | copy-start | bytes 393220

commit v2 on v1

--- a/solution.py
+++ b/solution.py
@@ -93,9 +93,12 @@
 
 
 def turns_kernel(
-    initial, forcing, current, cover, state, average,
+    initial_in, forcing_in, current_in, cover_in, state, average,
+    initial, forcing, current, cover,
     own, own_stat, halo, halo_stat, work, spare, stat, total, mean,
-    send, recv, stat_send, stat_recv, mean_send, mean_recv,
+    load, near_send, near_recv, far_send, far_recv,
+    stat_near_send, stat_near_recv, stat_far_send, stat_far_recv,
+    mean_send, mean_recv, go,
 ):
     me = lax.axis_index("blk")
     comp = lax.axis_index("comp")
@@ -103,62 +106,117 @@
     fields, rows, cols = initial.shape
     width = chunk_width(cols)
     chunks = cols // width
-    right, left = lax.rem(me + 1, count), lax.rem(me + count - 1, count)
-    has_left, has_right = me > 0, me < count - 1
+    near = 1 - lax.rem(me, 2)
+    far = 1 - near
+    partner = me + 2 * near - 1
+    relay_to = me + 4 * near - 2
+    relay_from = me - 4 * near + 2
+    can_send = jnp.logical_and(relay_to >= 0, relay_to < count)
+    can_recv = jnp.logical_and(relay_from >= 0, relay_from < count)
+    relay_to = lax.rem(relay_to + count, count)
+    relay_from = lax.rem(relay_from + count, count)
 
     barrier = pltpu.get_barrier_semaphore()
-    pl.semaphore_signal(barrier, inc=1, device_id={"blk": right}, device_id_type=MESH)
-    pl.semaphore_signal(barrier, inc=1, device_id={"blk": left}, device_id_type=MESH)
-    pl.semaphore_signal(barrier, inc=1, device_id={"comp": 1 - comp}, device_id_type=MESH)
+
+    def greet(where):
+        pl.semaphore_signal(barrier, inc=1, device_id=where, device_id_type=MESH)
+
+    greet({"blk": partner})
+    greet({"comp": 1 - comp})
+    pl.when(can_send)(lambda: greet({"blk": relay_to}))
+    pl.when(can_recv)(lambda: greet({"blk": relay_from}))
+    loads = [
+        pltpu.make_async_copy(source, target, load.at[i])
+        for i, (source, target) in enumerate(
+            (
+                (initial_in, initial),
+                (current_in, current),
+                (forcing_in, forcing),
+                (cover_in, cover),
+            )
+        )
+    ]
+    for copy in loads:
+        copy.start()
 
     work[...] = jnp.zeros_like(work)
-    spare[...] = jnp.zeros_like(spare)
     total[...] = jnp.zeros_like(total)
-    covered = cover[...].astype(jnp.float32)
-
-    def copies(source, target, out_sem, in_sem):
-        up = pltpu.make_async_remote_copy(
-            source, target.at[0], out_sem.at[0], in_sem.at[0],
-            device_id={"blk": right}, device_id_type=MESH,
-        )
-        down = pltpu.make_async_remote_copy(
-            source, target.at[1], out_sem.at[1], in_sem.at[1],
-            device_id={"blk": left}, device_id_type=MESH,
-        )
-        return up, down
+
+    def enter():
+        pl.semaphore_wait(barrier, 2 + can_send.astype(jnp.int32) + can_recv.astype(jnp.int32))
+
+    def copies(source, target, pieces, near_sems, far_sems):
+        first, second = [], []
+        for piece in range(pieces):
+            first.append(
+                pltpu.make_async_remote_copy(
+                    source.at[piece], target.at[far, piece],
+                    near_sems[0].at[piece], near_sems[1].at[piece],
+                    device_id={"blk": partner}, device_id_type=MESH,
+                )
+            )
+            second.append(
+                pltpu.make_async_remote_copy(
+                    target.at[near, piece], target.at[far, piece],
+                    far_sems[0].at[piece], far_sems[1].at[piece],
+                    device_id={"blk": relay_to}, device_id_type=MESH,
+                )
+            )
+        return first, second
 
     def start(pair):
-        pl.when(has_right)(pair[0].start)
-        pl.when(has_left)(pair[1].start)
+        for copy in pair[0]:
+            copy.start()
+
+    def relay(pair):
+        for first, second in zip(*pair):
+            first.wait_recv()
+            pl.when(can_send)(second.start)
 
     def arrive(pair):
-        pl.when(has_left)(pair[0].wait_recv)
-        pl.when(has_right)(pair[1].wait_recv)
+        @pl.when(can_recv)
+        def _():
+            for copy in pair[1]:
+                copy.wait_recv()
 
     def sent(pair):
-        pl.when(has_right)(pair[0].wait_send)
-        pl.when(has_left)(pair[1].wait_send)
+        for copy in pair[0]:
+            copy.wait_send()
+
+        @pl.when(can_send)
+        def _():
+            for copy in pair[1]:
+                copy.wait_send()
 
     def clear_edges(turns):
-        @pl.when(jnp.logical_not(has_left))
+        @pl.when(jnp.logical_not(can_recv))
         def _():
-            halo_stat[0] = jnp.zeros_like(halo_stat[0])
+            halo_stat[far] = jnp.zeros(halo_stat.shape[1:], jnp.float32)
             for turn in range(turns):
-                halo[turn, 0] = jnp.zeros_like(halo[turn, 0])
-
-        @pl.when(jnp.logical_not(has_right))
-        def _():
-            halo_stat[1] = jnp.zeros_like(halo_stat[1])
-            for turn in range(turns):
-                halo[turn, 1] = jnp.zeros_like(halo[turn, 1])
+                halo[turn, far] = jnp.zeros(halo.shape[2:], jnp.float32)
 
     inside = slice(PAD, PAD + cols)
 
-    def fill(turn, source):
+    def fill_own(source):
+        for field in range(fields):
+            work[field, rows : 2 * rows, inside] = source[field]
+
+    def fill_sides(turn):
         for field in range(fields):
             work[field, 0:rows, inside] = halo[turn, 0, field]
-            work[field, rows : 2 * rows, inside] = source[field]
             work[field, 2 * rows : 3 * rows, inside] = halo[turn, 1, field]
+
+    def exchange_of(turn, source):
+        return copies(
+            source, halo.at[turn], fields,
+            (near_send.at[turn], near_recv.at[turn]), (far_send.at[turn], far_recv.at[turn]),
+        )
+
+    def stats_of(source, pieces):
+        return copies(
+            source, halo_stat, pieces,
+            (stat_near_send, stat_near_recv), (stat_far_send, stat_far_recv),
+        )
 
     mean_copy = pltpu.make_async_remote_copy(
         mean, average, mean_send, mean_recv,
@@ -170,20 +228,33 @@
         depth = rows // 2
         turns = SUBCYCLES // depth
         clear_edges(turns)
+        loads[0].wait()
+        enter()
+        pairs = [exchange_of(0, initial)]
+        start(pairs[0])
+        for copy in loads[1:]:
+            copy.wait()
+        covered = cover[...].astype(jnp.float32)
         push = covered / (inertia * forcing[0] + 1.0)
         own_stat[0] = forcing[1] * covered * (1.0 / 3.0)
         own_stat[1] = push
         own_stat[2] = push * (forcing[2] + current[0])
         own_stat[3] = push * (forcing[3] + current[1])
-        pl.semaphore_wait(barrier, 3)
-        stat_pair = copies(own_stat, halo_stat, stat_send, stat_recv)
+        stat_pair = stats_of(own_stat, 4)
         start(stat_pair)
-        pairs = []
         for turn in range(turns):
             source = initial if turn == 0 else own.at[turn - 1]
-            pair = copies(source, halo.at[turn], send.at[turn], recv.at[turn])
-            pairs.append(pair)
-            start(pair)
+            if turn > 0:
+                pairs.append(exchange_of(turn, source))
+                start(pairs[turn])
+            relay(pairs[turn])
+            if turn == 0:
+                relay(stat_pair)
+                pl.semaphore_signal(
+                    go, inc=1, device_id={"comp": 1 - comp}, device_id_type=MESH
+                )
+            fill_own(source)
+            arrive(pairs[turn])
             if turn == 0:
                 arrive(stat_pair)
                 for place, block in enumerate((halo_stat.at[0], own_stat, halo_stat.at[1])):
@@ -194,8 +265,7 @@
                     stat[2, span] = 0.25 * push
                     stat[3, span] = block[2]
                     stat[4, span] = block[3]
-            arrive(pair)
-            fill(turn, source)
+            fill_sides(turn)
 
             def subcycle(step, carry):
                 for chunk in range(chunks):
@@ -209,6 +279,7 @@
             for field in range(fields):
                 final[field] = work[field, rows : 2 * rows, inside]
         share = 1.0 / SUBCYCLES
+        covered = cover[...].astype(jnp.float32)
         mean[0] = total[0] * share - covered * current[0]
         mean[1] = total[1] * share - covered * current[1]
         mean[2] = forcing[4] * covered * (total[2] * share)
@@ -224,15 +295,25 @@
         depth = rows
         turns = SUBCYCLES // depth
         clear_edges(turns)
-        pl.semaphore_wait(barrier, 3)
-        stat_pair = copies(current, halo_stat.at[:, pl.ds(0, 2)], stat_send, stat_recv)
+        spare[...] = jnp.zeros_like(spare)
+        for copy in loads:
+            copy.wait()
+        enter()
+        pl.semaphore_wait(go, 1)
+        pairs = [exchange_of(0, initial)]
+        start(pairs[0])
+        stat_pair = stats_of(current, 2)
         start(stat_pair)
-        pairs = []
         for turn in range(turns):
             source = initial if turn == 0 else own.at[turn - 1]
-            pair = copies(source, halo.at[turn], send.at[turn], recv.at[turn])
-            pairs.append(pair)
-            start(pair)
+            if turn > 0:
+                pairs.append(exchange_of(turn, source))
+                start(pairs[turn])
+            relay(pairs[turn])
+            if turn == 0:
+                relay(stat_pair)
+            fill_own(source)
+            arrive(pairs[turn])
             if turn == 0:
                 arrive(stat_pair)
                 for place in range(3):
@@ -244,8 +325,7 @@
                             speed = halo_stat[place // 2, axis]
                         stat[2 * axis, span] = courant * jnp.maximum(speed, 0.0)
                         stat[2 * axis + 1, span] = courant * jnp.minimum(speed, 0.0)
-            arrive(pair)
-            fill(turn, source)
+            fill_sides(turn)
 
             def substeps(step, carry):
                 for chunk in range(chunks):
@@ -276,9 +356,13 @@
             jax.ShapeDtypeStruct((fields, rows, cols), f32),
             jax.ShapeDtypeStruct((3, rows, cols), f32),
         ),
-        in_specs=[vmem] * 4,
+        in_specs=[pl.BlockSpec(memory_space=pl.ANY)] * 4,
         out_specs=(vmem, vmem),
         scratch_shapes=[
+            pltpu.VMEM(initial.shape, f32),
+            pltpu.VMEM(forcing.shape, f32),
+            pltpu.VMEM(current.shape, f32),
+            pltpu.VMEM(cover.shape, cover.dtype),
             pltpu.VMEM((most, fields, rows, cols), f32),
             pltpu.VMEM((4, rows, cols), f32),
             pltpu.VMEM((most, 2, fields, rows, cols), f32),
@@ -288,10 +372,13 @@
             pltpu.VMEM((5, 3 * rows, cols), f32),
             pltpu.VMEM((3, rows, cols), f32),
             pltpu.VMEM((3, rows, cols), f32),
-            dma((most, 2)), dma((most, 2)), dma((2,)), dma((2,)), dma, dma,
+            dma((4,)),
+            dma((most, fields)), dma((most, fields)), dma((most, fields)), dma((most, fields)),
+            dma((4,)), dma((4,)), dma((4,)), dma((4,)),
+            dma, dma, pltpu.SemaphoreType.REGULAR,
         ],
         compiler_params=pltpu.CompilerParams(
-            collective_id=0, has_side_effects=True, vmem_limit_bytes=40 * 1024 * 1024
+            collective_id=0, has_side_effects=True
         ),
         name="turns",
     )(initial, forcing, current, cover)
@@ -376,32 +463,51 @@
     pl.semaphore_signal(barrier, inc=1, device_id={"blk": left}, device_id_type=MESH)
     pl.semaphore_signal(barrier, inc=1, device_id={"comp": 1 - comp}, device_id_type=MESH)
     pl.semaphore_wait(barrier, 3)
-    side = pltpu.make_async_remote_copy(
-        window, beside, side_send, side_recv,
-        device_id={"comp": 1 - comp}, device_id_type=MESH,
-    )
-    onward = pltpu.make_async_remote_copy(
-        carry, before, next_send, next_recv, device_id={"blk": right}, device_id_type=MESH
-    )
+    channels = window.shape[0]
+    sides, onward = [], []
+    for half in (1, 0):
+        for channel in range(channels):
+            sides.append(
+                pltpu.make_async_remote_copy(
+                    window.at[channel, half], beside.at[channel, half],
+                    side_send.at[half, channel], side_recv.at[half, channel],
+                    device_id={"comp": 1 - comp}, device_id_type=MESH,
+                )
+            )
+    for channel in range(channels):
+        onward.append(
+            pltpu.make_async_remote_copy(
+                carry.at[channel], before.at[channel],
+                next_send.at[channel], next_recv.at[channel],
+                device_id={"blk": right}, device_id_type=MESH,
+            )
+        )
 
     @pl.when(comp == 0)
     def _():
-        side.start()
+        for copy in sides:
+            copy.start()
         out_state[...] = state[...]
         out_pair[...] = average[...]
-        side.wait_send()
+        for copy in sides:
+            copy.wait_send()
 
     @pl.when(comp == 1)
     def _():
-        side.wait_recv()
-        carry[...] = window[:, 1] + beside[:, 1]
-        onward.start()
-        out_pair[...] = window[:, 0] + beside[:, 0]
+        for channel in range(channels):
+            sides[channel].wait_recv()
+            carry[channel] = window[channel, 1] + beside[channel, 1]
+            onward[channel].start()
+        for channel in range(channels):
+            sides[channels + channel].wait_recv()
+            out_pair[channel] = window[channel, 0] + beside[channel, 0]
         out_state[...] = state[...]
-        onward.wait_recv()
-        out_pair[...] += before[...]
+        for channel in range(channels):
+            onward[channel].wait_recv()
+            out_pair[channel] += before[channel]
         out_state[0] -= dilution * out_pair[2]
-        onward.wait_send()
+        for channel in range(channels):
+            onward[channel].wait_send()
 
 
 def run_join(window, state, average):
@@ -420,7 +526,7 @@
             pltpu.VMEM(window.shape, jnp.float32),
             pltpu.VMEM(average.shape, jnp.float32),
             pltpu.VMEM(average.shape, jnp.float32),
-            dma, dma, dma, dma,
+            dma((2, channels)), dma((2, channels)), dma((channels,)), dma((channels,)),
         ],
         compiler_params=pltpu.CompilerParams(
             collective_id=1, has_side_effects=True, vmem_limit_bytes=40 * 1024 * 1024

time: 104 us -> 79.3 us (0.76)
  the two profiles are of different devices: /device:TPU:11 before, /device:TPU:1 now
where the time goes in v2:
time: 79.3 us; the launch traced here: 79.2 us
  Pallas kernels  76.1 us (96%)
  local copies, waits for them, and re-layouts  2.34 us (3%)
    pallas_call x1, Pallas kernels, run_turns(): pl.pallas_call(turns_kernel, out_shape=(jax.ShapeDtypeStruct((fields, row...  54.5 us
    pallas_call x1, Pallas kernels, run_join(): pl.pallas_call(join_kernel, out_shape=(jax.ShapeDtypeStruct(state.shape,...  13.2 us
    pallas_call x1, Pallas kernels, run_remap(): pl.pallas_call(remap_kernel, out_shape=jax.ShapeDtypeStruct((channels, 2,...  8.42 us
    unnamed x12, local copies, waits for them, and re-layouts  2.34 us

profile of v2, /device:TPU:1, one launch (start us, length us, event | category | flops | bytes accessed | tf_op | source)
XLA Modules:
  0.0 79.2 jit_solution(7021469635035083988)
XLA Ops:
  0.6 0.0 copy-start.3
  0.6 0.0 copy-start.4
  0.7 54.5 %turns.1 = (f32[5,8,2048]{2,1,0:T(8,128)}, f32[3,8,2048]{2,1,0:T(8,128)}) custom-call(f32[5,8,2048]{2,1,0:T(8,128)} %bitcast.5, f32[5,8,2048]{2,1,0:T(8,128)} %forcing_in.1, f32[2,8,2048]{2,1,0:T(8,128)} %current_in.1, s32[8,2048]{1,0:T(8,128)} %cover_in.1), custom_call_target="tpu_custom_call" | custom-call | tf_op jit(solution)/shard_map/turns/pallas_call | solution.py:353
  55.2 0.0 copy-done.3
  55.2 0.0 copy-done.4
  55.2 0.0 copy-start
  55.2 0.9 %copy-done = f32[3,8,2048]{2,1,0:T(8,128)S(1)} copy-done((f32[3,8,2048]{2,1,0:T(8,128)S(1)}, f32[3,8,2048]{2,1,0:T(8,128)}, u32[]{:S(2)}) %copy-start) | copy-done | bytes 196632
  56.1 0.0 copy-start.1
  56.1 0.0 copy-start.2
  56.1 8.4 %remap.1.window = f32[3,2,8,2048]{3,2,1,0:T(8,128)S(1)} custom-call(f32[3,8,2048]{2,1,0:T(8,128)S(1)} %copy-done, s32[2,8,2048]{2,1,0:T(8,128)S(1)} %copy-done.3, s32[2,8,2048]{2,1,0:T(8,128)S(1)} %copy-done.4), custom_call_target="tpu_custom_call" | custom-call | tf_op jit(solution)/shard_map/remap/pallas_call | solution.py:438
  64.5 0.0 copy-done.1
  64.5 0.0 copy-done.2
  64.6 13.2 %join.1 = (f32[5,8,2048]{2,1,0:T(8,128)S(1)}, f32[3,8,2048]{2,1,0:T(8,128)S(1)}) custom-call(f32[3,2,8,2048]{3,2,1,0:T(8,128)S(1)} %remap.1.window, f32[5,8,2048]{2,1,0:T(8,128)S(1)} %copy-done.2, f32[3,8,2048]{2,1,0:T(8,128)S(1)} %copy-done.1), custom_call_target="tpu_custom_call" | custom-call | tf_op jit(solution)/shard_map/join/pallas_call | solution.py:517
  77.8 0.7 copy.10
  78.5 0.7 copy.11
Async XLA Ops:
  0.6 54.5 %copy-start.3 = (s32[2,8,2048]{2,1,0:T(8,128)S(1)}, s32[2,8,2048]{2,1,0:T(8,128)}, u32[]{:S(2)}) copy-start(s32[2,8,2048]{2,1,0:T(8,128)} %targets.1) | copy-start | bytes 393220
  0.6 54.5 %copy-start.4 = (s32[2,8,2048]{2,1,0:T(8,128)S(1)}, s32[2,8,2048]{2,1,0:T(8,128)}, u32[]{:S(2)}) copy-start(s32[2,8,2048]{2,1,0:T(8,128)} %weights.1) | copy-start | bytes 393220
  55.2 0.9 %copy-start = (f32[3,8,2048]{2,1,0:T(8,128)S(1)}, f32[3,8,2048]{2,1,0:T(8,128)}, u32[]{:S(2)}) copy-start(f32[3,8,2048]{2,1,0:T(8,128)} %get-tuple-element.6.average) | copy-start | bytes 589828
  56.1 8.4 %copy-start.1 = (f32[3,8,2048]{2,1,0:T(8,128)S(1)}, f32[3,8,2048]{2,1,0:T(8,128)}, u32[]{:S(2)}) copy-start(f32[3,8,2048]{2,1,0:T(8,128)} %get-tuple-element.6.average) | copy-start | bytes 589828
  56.1 8.4 %copy-start.2 = (f32[5,8,2048]{2,1,0:T(8,128)S(1)}, f32[5,8,2048]{2,1,0:T(8,128)}, u32[]{:S(2)}) copy-start(f32[5,8,2048]{2,1,0:T(8,128)} %get-tuple-element.7.state) | copy-start | bytes 983044

commit v3 on v2

--- a/solution.py
+++ b/solution.py
@@ -10,6 +10,7 @@
 SUBCYCLES = 16
 MESH = pl.DeviceIdType.MESH
 PAD = 128
+PARTS = 2
 
 coriolis = 0.1
 inertia = 4.0
@@ -147,18 +148,20 @@
 
     def copies(source, target, pieces, near_sems, far_sems):
         first, second = [], []
-        for piece in range(pieces):
+        wide = cols // PARTS
+        for index in range(pieces * PARTS):
+            piece, place = index // PARTS, pl.ds(index % PARTS * wide, wide)
             first.append(
                 pltpu.make_async_remote_copy(
-                    source.at[piece], target.at[far, piece],
-                    near_sems[0].at[piece], near_sems[1].at[piece],
+                    source.at[piece, :, place], target.at[far, piece, :, place],
+                    near_sems[0].at[index], near_sems[1].at[index],
                     device_id={"blk": partner}, device_id_type=MESH,
                 )
             )
             second.append(
                 pltpu.make_async_remote_copy(
-                    target.at[near, piece], target.at[far, piece],
-                    far_sems[0].at[piece], far_sems[1].at[piece],
+                    target.at[near, piece, :, place], target.at[far, piece, :, place],
+                    far_sems[0].at[index], far_sems[1].at[index],
                     device_id={"blk": relay_to}, device_id_type=MESH,
                 )
             )
@@ -373,8 +376,8 @@
             pltpu.VMEM((3, rows, cols), f32),
             pltpu.VMEM((3, rows, cols), f32),
             dma((4,)),
-            dma((most, fields)), dma((most, fields)), dma((most, fields)), dma((most, fields)),
-            dma((4,)), dma((4,)), dma((4,)), dma((4,)),
+            *[dma((most, fields * PARTS)) for _ in range(4)],
+            *[dma((4 * PARTS,)) for _ in range(4)],
             dma, dma, pltpu.SemaphoreType.REGULAR,
         ],
         compiler_params=pltpu.CompilerParams(

time: 79.3 us -> 79.1 us (level)
  no operation moved by 1% of the time
where the time goes in v3:
time: 79.1 us; the launch traced here: 79 us
  Pallas kernels  75.9 us (96%)
  local copies, waits for them, and re-layouts  2.34 us (3%)
    pallas_call x1, Pallas kernels, run_turns(): pl.pallas_call(turns_kernel, out_shape=(jax.ShapeDtypeStruct((fields, row...  54.6 us
    pallas_call x1, Pallas kernels, run_join(): pl.pallas_call(join_kernel, out_shape=(jax.ShapeDtypeStruct(state.shape,...  12.9 us
    pallas_call x1, Pallas kernels, run_remap(): pl.pallas_call(remap_kernel, out_shape=jax.ShapeDtypeStruct((channels, 2,...  8.41 us
    unnamed x12, local copies, waits for them, and re-layouts  2.34 us

profile of v3, /device:TPU:1, one launch (start us, length us, event | category | flops | bytes accessed | tf_op | source)
XLA Modules:
  0.0 79.0 jit_solution(16105007502609251574)
XLA Ops:
  0.6 0.0 copy-start.3
  0.6 0.0 copy-start.4
  0.7 54.6 %turns.1 = (f32[5,8,2048]{2,1,0:T(8,128)}, f32[3,8,2048]{2,1,0:T(8,128)}) custom-call(f32[5,8,2048]{2,1,0:T(8,128)} %bitcast.5, f32[5,8,2048]{2,1,0:T(8,128)} %forcing_in.1, f32[2,8,2048]{2,1,0:T(8,128)} %current_in.1, s32[8,2048]{1,0:T(8,128)} %cover_in.1), custom_call_target="tpu_custom_call" | custom-call | tf_op jit(solution)/shard_map/turns/pallas_call | solution.py:356
  55.3 0.0 copy-done.3
  55.3 0.0 copy-done.4
  55.3 0.0 copy-start
  55.3 0.9 %copy-done = f32[3,8,2048]{2,1,0:T(8,128)S(1)} copy-done((f32[3,8,2048]{2,1,0:T(8,128)S(1)}, f32[3,8,2048]{2,1,0:T(8,128)}, u32[]{:S(2)}) %copy-start) | copy-done | bytes 196632
  56.2 0.0 copy-start.1
  56.2 0.0 copy-start.2
  56.2 8.4 %remap.1.window = f32[3,2,8,2048]{3,2,1,0:T(8,128)S(1)} custom-call(f32[3,8,2048]{2,1,0:T(8,128)S(1)} %copy-done, s32[2,8,2048]{2,1,0:T(8,128)S(1)} %copy-done.3, s32[2,8,2048]{2,1,0:T(8,128)S(1)} %copy-done.4), custom_call_target="tpu_custom_call" | custom-call | tf_op jit(solution)/shard_map/remap/pallas_call | solution.py:441
  64.7 0.0 copy-done.1
  64.7 0.0 copy-done.2
  64.7 12.9 %join.1 = (f32[5,8,2048]{2,1,0:T(8,128)S(1)}, f32[3,8,2048]{2,1,0:T(8,128)S(1)}) custom-call(f32[3,2,8,2048]{3,2,1,0:T(8,128)S(1)} %remap.1.window, f32[5,8,2048]{2,1,0:T(8,128)S(1)} %copy-done.2, f32[3,8,2048]{2,1,0:T(8,128)S(1)} %copy-done.1), custom_call_target="tpu_custom_call" | custom-call | tf_op jit(solution)/shard_map/join/pallas_call | solution.py:520
  77.6 0.7 copy.10
  78.3 0.7 copy.11
Async XLA Ops:
  0.6 54.7 %copy-start.3 = (s32[2,8,2048]{2,1,0:T(8,128)S(1)}, s32[2,8,2048]{2,1,0:T(8,128)}, u32[]{:S(2)}) copy-start(s32[2,8,2048]{2,1,0:T(8,128)} %targets.1) | copy-start | bytes 393220
  0.6 54.7 %copy-start.4 = (s32[2,8,2048]{2,1,0:T(8,128)S(1)}, s32[2,8,2048]{2,1,0:T(8,128)}, u32[]{:S(2)}) copy-start(s32[2,8,2048]{2,1,0:T(8,128)} %weights.1) | copy-start | bytes 393220
  55.3 0.9 %copy-start = (f32[3,8,2048]{2,1,0:T(8,128)S(1)}, f32[3,8,2048]{2,1,0:T(8,128)}, u32[]{:S(2)}) copy-start(f32[3,8,2048]{2,1,0:T(8,128)} %get-tuple-element.6.average) | copy-start | bytes 589828
  56.2 8.4 %copy-start.1 = (f32[3,8,2048]{2,1,0:T(8,128)S(1)}, f32[3,8,2048]{2,1,0:T(8,128)}, u32[]{:S(2)}) copy-start(f32[3,8,2048]{2,1,0:T(8,128)} %get-tuple-element.6.average) | copy-start | bytes 589828
  56.2 8.4 %copy-start.2 = (f32[5,8,2048]{2,1,0:T(8,128)S(1)}, f32[5,8,2048]{2,1,0:T(8,128)}, u32[]{:S(2)}) copy-start(f32[5,8,2048]{2,1,0:T(8,128)} %get-tuple-element.7.state) | copy-start | bytes 983044
